TPU v7x, 32 devices: a whole 2x2x4 slice. The times are simulated.
32 devices in a mesh: freq: 4 (over y, core), stn: 8 (over z, x).
Axes of the slice: x: 2, y: 2, z: 4, core: 2. Of those that a mesh axis runs over, the one named last changes fastest.
Arguments:
- samples: bfloat16 [4, 256, 24, 2, 128], P('freq', 'stn'), may hold values from -8 to 8, as said below
- window: float32 [128], replicated, may hold values from 0.1 to 1
- group_of_device: int32 [8], replicated, may hold values from 0 to 7, each once
- owner_map: int32 [8, 8], replicated, may hold values from 0 to 7, as said below
Outputs:
- owned: bfloat16 [2, 32, 8, 8, 1024], P(None, None, 'stn', 'freq')
Inputs may be any that keep to these rules, and one draw needn't show every extreme that they name: `samples`: samples are finite and bounded. Every row and every column of owner_map names each stn index exactly once.
All inputs are finite; a program needn't handle non-finite values.
Results may differ from a plain program's by a relative error of at most 0.0065.
Values may be sent and summed in bfloat16 or wider, within the bound.
A program may use at most 64 MiB of HBM per device.

v0:
```python
import functools
import math

import jax
import jax.numpy as jnp
import numpy as np
from jax import lax
from jax.experimental import pallas as pl
from jax.experimental.pallas import tpu as pltpu
from jax.sharding import PartitionSpec as P

AVG = 16
LANES = 128
MESH = pl.DeviceIdType.MESH
OUT_SPACE = pltpu.VMEM


def swap_blocks(blocks, width):
    blocks = list(blocks)
    count = len(blocks)
    lane = lax.broadcasted_iota(jnp.int32, blocks[0].shape, 1) // width
    step = count // 2
    while step:
        upper = (lane // step) % 2 == 1
        for i in range(count):
            if (i // step) % 2 == 0:
                u, v = blocks[i], blocks[i + step]
                shift = step * width
                blocks[i] = jnp.where(upper, pltpu.roll(v, shift, 1), u)
                blocks[i + step] = jnp.where(upper, v, pltpu.roll(u, LANES - shift, 1))
        step //= 2
    return blocks


def kernel(
    nf, ns, rows, spec,
    x_hbm, w_hbm, trig_hbm, god_hbm, own_hbm,
    out_ref,
    x_ref, w_ref, trig_ref, god_ref, own_ref,
    xf, send1, held, left, vis, tiles, mixed, send2, dev_of, table,
    lsem, row_sem, ssem1, rsem1, ssem2, rsem2,
):
    length = LANES
    ch_out = length // AVG
    spread = ns // ch_out
    rpf = ns // nf
    fl_count = ch_out // rpf
    chunks = spec // ch_out
    step = 2 * ch_out
    b = lax.axis_index("freq")
    me = lax.axis_index("stn")

    def load(n, src, dst):
        return pltpu.make_async_copy(src, dst, lsem.at[n])

    def load_x(th):
        return load(4 + th, x_hbm.at[:, th * step : (th + 1) * step, :], x_ref.at[th])

    load_w = load(0, w_hbm, w_ref)
    load_trig = load(1, trig_hbm, trig_ref)
    load_god = load(2, god_hbm, god_ref)
    load_own = load(3, own_hbm, own_ref)
    load_w.start()
    load_trig.start()
    for th in range(chunks):
        load_x(th).start()
    load_god.start()
    load_own.start()

    barrier = pltpu.get_barrier_semaphore()
    offsets = sorted(range(1, ns), key=lambda o: abs(o - ns / 2))
    for off in offsets:
        pl.semaphore_signal(
            barrier, inc=1, device_id=(b, lax.rem(me + off, ns)), device_id_type=MESH
        )
    for off in range(1, nf):
        pl.semaphore_signal(
            barrier, inc=1, device_id=(lax.rem(b + off, nf), me), device_id_type=MESH
        )

    load_w.wait()
    load_trig.wait()
    weights = jnp.broadcast_to(w_ref[...], (length, length)).T * (1.0 / math.sqrt(length))
    cosine = weights * trig_ref[0]
    sine = weights * trig_ref[1]
    matrix = jnp.concatenate(
        [jnp.concatenate([cosine, -sine], axis=1), jnp.concatenate([sine, cosine], axis=1)], axis=0
    )
    high = matrix.astype(jnp.bfloat16)
    low = (matrix - high.astype(jnp.float32)).astype(jnp.bfloat16)

    for th in range(chunks):
        load_x(th).wait()
    for th in range(chunks):
        xf[th] = x_ref[th].astype(jnp.float32).reshape(rows * step, length)
    for th in range(chunks):
        parts = []
        for t in range(ch_out):
            re = xf[th, pl.ds(2 * t, rows, stride=step), :]
            im = xf[th, pl.ds(2 * t + 1, rows, stride=step), :]
            parts.append(jnp.concatenate([re, im], axis=1).astype(jnp.bfloat16))
        flat = jnp.concatenate(parts, axis=0)
        spectra = jnp.dot(flat, high, preferred_element_type=jnp.float32) + jnp.dot(
            flat, low, preferred_element_type=jnp.float32
        )
        for p in range(2):
            blocks = [
                spectra[i * rows : (i + 1) * rows, p * LANES : (p + 1) * LANES]
                for i in range(ch_out)
            ]
            blocks = swap_blocks(blocks, AVG)
            for k in range(ch_out):
                send1[k, th, :, p * LANES : (p + 1) * LANES] = blocks[k].astype(jnp.bfloat16)

    def first_copy(d, mine):
        return pltpu.make_async_remote_copy(
            src_ref=send1.at[d // spread],
            dst_ref=held.at[mine],
            send_sem=ssem1.at[d],
            recv_sem=rsem1.at[mine],
            device_id=(b, d),
            device_id_type=MESH,
        )

    pl.semaphore_wait(barrier, ns - 1 + nf - 1)
    for off in offsets:
        first_copy(lax.rem(me + off, ns), me).start()

    for off in range(1, nf):
        pl.semaphore_signal(
            row_sem, inc=1, device_id=(lax.rem(b + off, nf), me), device_id_type=MESH
        )
    held[me] = send1[me // spread]

    load_god.wait()
    load_own.wait()

    def find_dev(g, carry):
        def body(s, acc):
            return jnp.where(god_ref[s] == g, s, acc)

        dev_of[g] = lax.fori_loop(0, ns, body, jnp.int32(0), unroll=min(ns, 8))
        return carry

    lax.fori_loop(0, ns, find_dev, 0)
    quarter = lax.rem(me, spread)

    def find_col(i, carry):
        g1 = quarter * ch_out + i // ns
        o = lax.rem(i, ns)

        def body(g2, acc):
            return jnp.where(own_ref[g1, g2] == o, dev_of[g2], acc)

        table[i] = lax.fori_loop(0, ns, body, jnp.int32(0), unroll=min(ns, 8))
        return carry

    lax.fori_loop(0, ch_out * ns, find_col, 0)
    pl.semaphore_wait(row_sem, nf - 1)

    channel = b * ch_out + me // spread
    first_row = quarter * fl_count

    def second_copy(fl, o):
        return pltpu.make_async_remote_copy(
            src_ref=send2.at[fl * ns + o],
            dst_ref=out_ref.at[:, channel],
            send_sem=ssem2.at[fl * ns + o],
            recv_sem=rsem2.at[channel],
            device_id=(first_row + fl, o),
            device_id_type=MESH,
        )

    def unless_mine(fl, o, run):
        mine = jnp.logical_and(first_row + fl == b, o == me)
        pl.when(jnp.logical_not(mine))(run)

    per_tile = LANES // rows
    sub = rows // per_tile
    span = rpf * rows
    wide = min(2 * per_tile, ns)
    cols = wide * rows

    def wait_first(i, carry):
        first_copy(me, lax.rem(me + i, ns)).wait_recv()
        return carry

    lax.fori_loop(1, ns, wait_first, 0)

    for fl in range(fl_count):
        for g in range(rpf):
            x = held[dev_of[(first_row + fl) * rpf + g]]
            for th in range(chunks):
                left[th, g * rows : (g + 1) * rows, :] = x[th]
                left[th, span + g * rows : span + (g + 1) * rows, :LANES] = x[th, :, LANES:]
                left[th, span + g * rows : span + (g + 1) * rows, LANES:] = -x[th, :, :LANES]
        for c in range(ns // wide):
            block = sum(
                lax.dot_general(
                    left[th],
                    held[c * wide : (c + 1) * wide, th].reshape(cols, 2 * LANES),
                    (((1,), (1,)), ((), ())),
                    preferred_element_type=jnp.float32,
                )
                for th in range(chunks)
            ) * (1.0 / (AVG * spec))
            for h in range(cols // LANES):
                vis[h] = block[:, h * LANES : (h + 1) * LANES]
            for h in range(cols // LANES):
                blocks = [
                    vis[h, pl.ds(q, 2 * span // per_tile, stride=per_tile), :]
                    for q in range(per_tile)
                ]
                blocks = swap_blocks(blocks, rows)
                for s in range(per_tile):
                    tiles[c * wide + h * per_tile + s] = blocks[s].reshape(2 * rpf, sub, LANES)

        def build(o, carry):
            for g in range(rpf):
                source = table[(fl * rpf + g) * ns + o]
                for p in range(2):
                    mixed[o, p, pl.ds(g, sub, stride=rpf), :] = tiles[source, p * rpf + g]
            for p in range(2):
                for r in range(sub):
                    send2[fl * ns + o, p, :, r * LANES : (r + 1) * LANES] = mixed[
                        o, p, r * rpf : (r + 1) * rpf, :
                    ].astype(jnp.bfloat16)
            unless_mine(fl, o, lambda: second_copy(fl, o).start())
            return carry

        lax.fori_loop(0, ns, build, 0, unroll=min(ns, 8))

    own_here = quarter == b // fl_count

    @pl.when(own_here)
    def _():
        own = pltpu.make_async_copy(
            send2.at[lax.rem(b, fl_count) * ns + me], out_ref.at[:, channel], lsem.at[0]
        )
        own.start()
        own.wait()

    def wait_first_send(i, carry):
        first_copy(lax.rem(me + i, ns), me).wait_send()
        return carry

    lax.fori_loop(1, ns, wait_first_send, 0)

    def arrived(slot):
        pltpu.make_async_remote_copy(
            src_ref=send2.at[0],
            dst_ref=out_ref.at[:, slot],
            send_sem=ssem2.at[0],
            recv_sem=rsem2.at[slot],
            device_id=(b, me),
            device_id_type=MESH,
        ).wait_recv()

    def wait_arrival(i, carry):
        arrived(lax.rem(channel + i, nf * ch_out))
        return carry

    pl.when(jnp.logical_not(own_here))(lambda: arrived(channel))
    lax.fori_loop(1, nf * ch_out, wait_arrival, 0)

    def wait_second(i, carry):
        fl, o = i // ns, lax.rem(i, ns)
        unless_mine(fl, o, lambda: second_copy(fl, o).wait_send())
        return carry

    lax.fori_loop(0, fl_count * ns, wait_second, 0)


def shards(nf, ns, samples, window, group_of_device, owner_map):
    _, rows, spec, _, length = samples.shape
    ch_out = length // AVG
    rpf = ns // nf
    fl_count = ch_out // rpf
    per_tile = LANES // rows
    sub = rows // per_tile
    chunks = spec // ch_out
    index = np.arange(length)
    theta = (index[:, None] * index[None, :] % length) * (2.0 * math.pi / length)
    trig = jnp.asarray(np.stack([np.cos(theta), np.sin(theta)]), jnp.float32)
    x = samples.reshape(rows, spec * 2, length)
    hbm = pl.BlockSpec(memory_space=pltpu.HBM)
    out = pl.pallas_call(
        functools.partial(kernel, nf, ns, rows, spec),
        out_shape=pltpu.VMEM((2, nf * ch_out, rpf, sub * LANES), jnp.bfloat16),
        in_specs=[hbm] * 5,
        out_specs=pl.BlockSpec(memory_space=OUT_SPACE),
        scratch_shapes=[
            pltpu.VMEM((chunks, rows, 2 * ch_out, length), jnp.bfloat16),
            pltpu.VMEM((1, length), jnp.float32),
            pltpu.VMEM((2, length, length), jnp.float32),
            pltpu.SMEM((ns,), jnp.int32),
            pltpu.SMEM((ns, ns), jnp.int32),
            pltpu.VMEM((chunks, rows * 2 * ch_out, length), jnp.float32),
            pltpu.VMEM((ch_out, chunks, rows, 2 * LANES), jnp.bfloat16),
            pltpu.VMEM((ns, chunks, rows, 2 * LANES), jnp.bfloat16),
            pltpu.VMEM((chunks, 2 * rpf * rows, 2 * LANES), jnp.bfloat16),
            pltpu.VMEM((2, 2 * rpf * rows, LANES), jnp.float32),
            pltpu.VMEM((ns, 2 * rpf, sub, LANES), jnp.float32),
            pltpu.VMEM((ns, 2, sub * rpf, LANES), jnp.float32),
            pltpu.VMEM((fl_count * ns, 2, rpf, sub * LANES), jnp.bfloat16),
            pltpu.SMEM((ns,), jnp.int32),
            pltpu.SMEM((ch_out * ns,), jnp.int32),
            pltpu.SemaphoreType.DMA((4 + chunks,)),
            pltpu.SemaphoreType.REGULAR,
            pltpu.SemaphoreType.DMA((ns,)),
            pltpu.SemaphoreType.DMA((ns,)),
            pltpu.SemaphoreType.DMA((fl_count * ns,)),
            pltpu.SemaphoreType.DMA((nf * ch_out,)),
        ],
        compiler_params=pltpu.CompilerParams(
            collective_id=0, has_side_effects=True, vmem_limit_bytes=60 * 1024 * 1024
        ),
    )(x, window.reshape(1, length), trig, group_of_device, owner_map)
    return out[:, :, None]


def solution(mesh):
    return jax.shard_map(
        functools.partial(shards, mesh.shape["freq"], mesh.shape["stn"]),
        mesh=mesh,
        in_specs=(P("freq", "stn", None, None, None), P(), P(), P()),
        out_specs=P(None, None, "stn", "freq", None),
        check_vma=False,
    )
```

profile of v0, /device:TPU:0, one launch (start us, length us, event | category | flops | bytes accessed | tf_op | source)
XLA Modules:
  0.0 23.2 jit_solution(11528304520619791029)
XLA Ops:
  0.0 22.5 %shard_map.55 = bf16[2,32,2,1024]{3,2,1,0:T(2,128)(2,1)S(1)} custom-call(bf16[32,48,128]{2,1,0:T(8,128)(2,1)} %bitcast.6, f32[1,128]{1,0:T(1,128)} %bitcast.7, f32[2,128,128]{2,1,0:T(8,128)} %constant.2.clone.trig_hbm, s32[8]{0:T(128)} %god_hbm.1, s32[8,8]{1,0:T(8,128)} %own_hbm.1), custom_call_target="tpu_custom_call" | custom-call | tf_op jit(solution)/shard_map/pallas_call | solution.py:287
  22.5 0.7 %copy.8 = bf16[2,32,1,2,1024]{4,3,2,1,0:T(2,128)(2,1)} copy(bf16[2,32,1,2,1024]{4,3,2,1,0:T(2,128)(2,1)S(1)} %bitcast.5) | data formatting | bytes 524288
where the time goes:
time: 23.4 us; the launch traced here: 23.2 us
  Pallas kernels  22.5 us (96%)
  local copies, waits for them, and re-layouts  0.71 us (3%)
    pallas_call x1, Pallas kernels, shards(): pl.pallas_call(functools.partial(kernel, nf, ns, rows, spec), out_shape=p...  22.5 us
    unnamed x1, local copies, waits for them, and re-layouts  0.71 us

commit v1 on v0

--- a/solution.py
+++ b/solution.py
@@ -11,25 +11,33 @@
 
 AVG = 16
 LANES = 128
+LEAD = 3
+HOLD = 1
+SLOW_EIGHTHS = (4, 3, 5, 2, 1, 6, 7)
+FAST_EIGHTHS = (4, 5, 3, 2, 6, 1, 7)
 MESH = pl.DeviceIdType.MESH
 OUT_SPACE = pltpu.VMEM
 
 
-def swap_blocks(blocks, width):
-    blocks = list(blocks)
+def orders(ns):
+    plans = []
+    for eighths in (SLOW_EIGHTHS, FAST_EIGHTHS):
+        plan = [e * ns // 8 + k for e in eighths for k in range(ns // 8)]
+        plans.append(plan + [off for off in range(1, ns) if off not in plan])
+    return plans
+
+
+def deal_blocks(blocks, width):
     count = len(blocks)
     lane = lax.broadcasted_iota(jnp.int32, blocks[0].shape, 1) // width
-    step = count // 2
-    while step:
+    turned = [pltpu.roll(x, i * width, 1) if i else x for i, x in enumerate(blocks)]
+    dealt = [turned[-k % count] for k in range(count)]
+    step = 1
+    while step < count:
         upper = (lane // step) % 2 == 1
-        for i in range(count):
-            if (i // step) % 2 == 0:
-                u, v = blocks[i], blocks[i + step]
-                shift = step * width
-                blocks[i] = jnp.where(upper, pltpu.roll(v, shift, 1), u)
-                blocks[i + step] = jnp.where(upper, v, pltpu.roll(u, LANES - shift, 1))
-        step //= 2
-    return blocks
+        dealt = [jnp.where(upper, dealt[(k - step) % count], dealt[k]) for k in range(count)]
+        step *= 2
+    return dealt
 
 
 def kernel(
@@ -38,7 +46,7 @@
     out_ref,
     x_ref, w_ref, trig_ref, god_ref, own_ref,
     xf, send1, held, left, vis, tiles, mixed, send2, dev_of, table,
-    lsem, row_sem, ssem1, rsem1, ssem2, rsem2,
+    lsem, row_sem, twin_sem, ssem1, rsem1, ssem2, rsem2,
 ):
     length = LANES
     ch_out = length // AVG
@@ -108,7 +116,7 @@
                 spectra[i * rows : (i + 1) * rows, p * LANES : (p + 1) * LANES]
                 for i in range(ch_out)
             ]
-            blocks = swap_blocks(blocks, AVG)
+            blocks = deal_blocks(blocks, AVG)
             for k in range(ch_out):
                 send1[k, th, :, p * LANES : (p + 1) * LANES] = blocks[k].astype(jnp.bfloat16)
 
@@ -123,8 +131,28 @@
         )
 
     pl.semaphore_wait(barrier, ns - 1 + nf - 1)
-    for off in offsets:
-        first_copy(lax.rem(me + off, ns), me).start()
+    def start_first(offs):
+        for off in offs:
+            first_copy(lax.rem(me + off, ns), me).start()
+
+    def end_first(offs):
+        for off in offs:
+            first_copy(lax.rem(me + off, ns), me).wait_send()
+
+    slow = lax.rem(b, 2) == 0
+    slow_order, fast_order = orders(ns)
+
+    @pl.when(slow)
+    def _():
+        start_first(slow_order)
+        end_first(slow_order[:LEAD])
+        pl.semaphore_signal(twin_sem, inc=1, device_id=(b + 1, me), device_id_type=MESH)
+
+    @pl.when(jnp.logical_not(slow))
+    def _():
+        start_first(fast_order[:HOLD])
+        pl.semaphore_wait(twin_sem, 1)
+        start_first(fast_order[HOLD:])
 
     for off in range(1, nf):
         pl.semaphore_signal(
@@ -187,48 +215,65 @@
 
     lax.fori_loop(1, ns, wait_first, 0)
 
-    for fl in range(fl_count):
-        for g in range(rpf):
-            x = held[dev_of[(first_row + fl) * rpf + g]]
-            for th in range(chunks):
-                left[th, g * rows : (g + 1) * rows, :] = x[th]
-                left[th, span + g * rows : span + (g + 1) * rows, :LANES] = x[th, :, LANES:]
-                left[th, span + g * rows : span + (g + 1) * rows, LANES:] = -x[th, :, :LANES]
+    pair = 2 - fl_count % 2
+    block_rows = 2 * span
+
+    def correlate(f0):
+        for u in range(pair):
+            top = u * block_rows
+            for g in range(rpf):
+                x = held[dev_of[(first_row + f0 + u) * rpf + g]]
+                at = top + g * rows
+                for th in range(chunks):
+                    left[th, at : at + rows, :] = x[th]
+                    left[th, at + span : at + span + rows, :LANES] = x[th, :, LANES:]
+                    left[th, at + span : at + span + rows, LANES:] = -x[th, :, :LANES]
         for c in range(ns // wide):
-            block = sum(
-                lax.dot_general(
-                    left[th],
-                    held[c * wide : (c + 1) * wide, th].reshape(cols, 2 * LANES),
-                    (((1,), (1,)), ((), ())),
-                    preferred_element_type=jnp.float32,
-                )
-                for th in range(chunks)
-            ) * (1.0 / (AVG * spec))
-            for h in range(cols // LANES):
-                vis[h] = block[:, h * LANES : (h + 1) * LANES]
+            for u in range(pair):
+                block = sum(
+                    lax.dot_general(
+                        left[th, u * block_rows : (u + 1) * block_rows],
+                        held[c * wide : (c + 1) * wide, th].reshape(cols, 2 * LANES),
+                        (((1,), (1,)), ((), ())),
+                        preferred_element_type=jnp.float32,
+                    )
+                    for th in range(chunks)
+                ) * (1.0 / (AVG * spec))
+                for h in range(cols // LANES):
+                    vis[h, u * block_rows : (u + 1) * block_rows] = block[:, h * LANES : (h + 1) * LANES]
             for h in range(cols // LANES):
                 blocks = [
-                    vis[h, pl.ds(q, 2 * span // per_tile, stride=per_tile), :]
+                    vis[h, pl.ds(q, pair * block_rows // per_tile, stride=per_tile), :]
                     for q in range(per_tile)
                 ]
-                blocks = swap_blocks(blocks, rows)
+                blocks = deal_blocks(blocks, rows)
                 for s in range(per_tile):
-                    tiles[c * wide + h * per_tile + s] = blocks[s].reshape(2 * rpf, sub, LANES)
-
-        def build(o, carry):
-            for g in range(rpf):
-                source = table[(fl * rpf + g) * ns + o]
-                for p in range(2):
-                    mixed[o, p, pl.ds(g, sub, stride=rpf), :] = tiles[source, p * rpf + g]
+                    whole = pltpu.roll(blocks[s], LANES - s * rows, 1) if s else blocks[s]
+                    shaped = whole.reshape(pair, 2 * rpf, sub, LANES)
+                    for u in range(pair):
+                        tiles[f0 + u, c * wide + h * per_tile + s] = shaped[u]
+
+    def build(fl, o):
+        for g in range(rpf):
+            source = table[(fl * rpf + g) * ns + o]
             for p in range(2):
-                for r in range(sub):
-                    send2[fl * ns + o, p, :, r * LANES : (r + 1) * LANES] = mixed[
-                        o, p, r * rpf : (r + 1) * rpf, :
-                    ].astype(jnp.bfloat16)
-            unless_mine(fl, o, lambda: second_copy(fl, o).start())
+                mixed[fl, o, p, pl.ds(g, sub, stride=rpf), :] = tiles[fl, source, p * rpf + g]
+        for p in range(2):
+            for r in range(sub):
+                send2[fl * ns + o, p, :, r * LANES : (r + 1) * LANES] = mixed[
+                    fl, o, p, r * rpf : (r + 1) * rpf, :
+                ].astype(jnp.bfloat16)
+        unless_mine(fl, o, lambda: second_copy(fl, o).start())
+
+    for f0 in range(0, fl_count, pair):
+        correlate(f0)
+
+        def build_owner(o, carry):
+            for u in range(pair):
+                build(f0 + u, o)
             return carry
 
-        lax.fori_loop(0, ns, build, 0, unroll=min(ns, 8))
+        lax.fori_loop(0, ns, build_owner, 0, unroll=min(ns, 8))
 
     own_here = quarter == b // fl_count
 
@@ -240,11 +285,8 @@
         own.start()
         own.wait()
 
-    def wait_first_send(i, carry):
-        first_copy(lax.rem(me + i, ns), me).wait_send()
-        return carry
-
-    lax.fori_loop(1, ns, wait_first_send, 0)
+    pl.when(slow)(lambda: end_first(slow_order[LEAD:]))
+    pl.when(jnp.logical_not(slow))(lambda: end_first(fast_order))
 
     def arrived(slot):
         pltpu.make_async_remote_copy(
@@ -298,14 +340,15 @@
             pltpu.VMEM((chunks, rows * 2 * ch_out, length), jnp.float32),
             pltpu.VMEM((ch_out, chunks, rows, 2 * LANES), jnp.bfloat16),
             pltpu.VMEM((ns, chunks, rows, 2 * LANES), jnp.bfloat16),
-            pltpu.VMEM((chunks, 2 * rpf * rows, 2 * LANES), jnp.bfloat16),
-            pltpu.VMEM((2, 2 * rpf * rows, LANES), jnp.float32),
-            pltpu.VMEM((ns, 2 * rpf, sub, LANES), jnp.float32),
-            pltpu.VMEM((ns, 2, sub * rpf, LANES), jnp.float32),
+            pltpu.VMEM((chunks, 4 * rpf * rows, 2 * LANES), jnp.bfloat16),
+            pltpu.VMEM((2, 4 * rpf * rows, LANES), jnp.float32),
+            pltpu.VMEM((fl_count, ns, 2 * rpf, sub, LANES), jnp.float32),
+            pltpu.VMEM((fl_count, ns, 2, sub * rpf, LANES), jnp.float32),
             pltpu.VMEM((fl_count * ns, 2, rpf, sub * LANES), jnp.bfloat16),
             pltpu.SMEM((ns,), jnp.int32),
             pltpu.SMEM((ch_out * ns,), jnp.int32),
             pltpu.SemaphoreType.DMA((4 + chunks,)),
+            pltpu.SemaphoreType.REGULAR,
             pltpu.SemaphoreType.REGULAR,
             pltpu.SemaphoreType.DMA((ns,)),
             pltpu.SemaphoreType.DMA((ns,)),

time: 23.4 us -> 23 us (0.983)
  the two profiles are of different devices: /device:TPU:0 before, /device:TPU:7 now
where the time goes in v1:
time: 23 us; the launch traced here: 22.8 us
  Pallas kernels  22.1 us (96%)
  local copies, waits for them, and re-layouts  0.71 us (3%)
    pallas_call x1, Pallas kernels, shards(): pl.pallas_call(functools.partial(kernel, nf, ns, rows, spec), out_shape=p...  22.1 us
    unnamed x1, local copies, waits for them, and re-layouts  0.71 us

profile of v1, /device:TPU:7, one launch (start us, length us, event | category | flops | bytes accessed | tf_op | source)
XLA Modules:
  0.0 22.8 jit_solution(16254945607188021585)
XLA Ops:
  0.0 22.1 %shard_map.55 = bf16[2,32,2,1024]{3,2,1,0:T(2,128)(2,1)S(1)} custom-call(bf16[32,48,128]{2,1,0:T(8,128)(2,1)} %bitcast.6, f32[1,128]{1,0:T(1,128)} %bitcast.7, f32[2,128,128]{2,1,0:T(8,128)} %constant.2.clone.trig_hbm, s32[8]{0:T(128)} %god_hbm.1, s32[8,8]{1,0:T(8,128)} %own_hbm.1), custom_call_target="tpu_custom_call" | custom-call | tf_op jit(solution)/shard_map/pallas_call | solution.py:329
  22.1 0.7 %copy.8 = bf16[2,32,1,2,1024]{4,3,2,1,0:T(2,128)(2,1)} copy(bf16[2,32,1,2,1024]{4,3,2,1,0:T(2,128)(2,1)S(1)} %bitcast.5) | data formatting | bytes 524288

commit v2 on v1

--- a/solution.py
+++ b/solution.py
@@ -120,12 +120,15 @@
             for k in range(ch_out):
                 send1[k, th, :, p * LANES : (p + 1) * LANES] = blocks[k].astype(jnp.bfloat16)
 
+    def whole(ref, sem):
+        return pltpu.make_async_copy(ref, ref, sem.at[0])
+
     def first_copy(d, mine):
         return pltpu.make_async_remote_copy(
             src_ref=send1.at[d // spread],
             dst_ref=held.at[mine],
             send_sem=ssem1.at[d],
-            recv_sem=rsem1.at[mine],
+            recv_sem=rsem1.at[0],
             device_id=(b, d),
             device_id_type=MESH,
         )
@@ -193,8 +196,8 @@
         return pltpu.make_async_remote_copy(
             src_ref=send2.at[fl * ns + o],
             dst_ref=out_ref.at[:, channel],
-            send_sem=ssem2.at[fl * ns + o],
-            recv_sem=rsem2.at[channel],
+            send_sem=ssem2.at[0],
+            recv_sem=rsem2.at[0],
             device_id=(first_row + fl, o),
             device_id_type=MESH,
         )
@@ -209,11 +212,7 @@
     wide = min(2 * per_tile, ns)
     cols = wide * rows
 
-    def wait_first(i, carry):
-        first_copy(me, lax.rem(me + i, ns)).wait_recv()
-        return carry
-
-    lax.fori_loop(1, ns, wait_first, 0)
+    whole(held.at[: ns - 1], rsem1).wait()
 
     pair = 2 - fl_count % 2
     block_rows = 2 * span
@@ -288,29 +287,12 @@
     pl.when(slow)(lambda: end_first(slow_order[LEAD:]))
     pl.when(jnp.logical_not(slow))(lambda: end_first(fast_order))
 
-    def arrived(slot):
-        pltpu.make_async_remote_copy(
-            src_ref=send2.at[0],
-            dst_ref=out_ref.at[:, slot],
-            send_sem=ssem2.at[0],
-            recv_sem=rsem2.at[slot],
-            device_id=(b, me),
-            device_id_type=MESH,
-        ).wait_recv()
-
-    def wait_arrival(i, carry):
-        arrived(lax.rem(channel + i, nf * ch_out))
-        return carry
-
-    pl.when(jnp.logical_not(own_here))(lambda: arrived(channel))
-    lax.fori_loop(1, nf * ch_out, wait_arrival, 0)
-
-    def wait_second(i, carry):
-        fl, o = i // ns, lax.rem(i, ns)
-        unless_mine(fl, o, lambda: second_copy(fl, o).wait_send())
-        return carry
-
-    lax.fori_loop(0, fl_count * ns, wait_second, 0)
+    def end_second(count):
+        whole(send2.at[:count], ssem2).wait()
+        whole(out_ref.at[:, :count], rsem2).wait()
+
+    pl.when(own_here)(lambda: end_second(nf * ch_out - 1))
+    pl.when(jnp.logical_not(own_here))(lambda: end_second(nf * ch_out))
 
 
 def shards(nf, ns, samples, window, group_of_device, owner_map):
@@ -351,9 +333,9 @@
             pltpu.SemaphoreType.REGULAR,
             pltpu.SemaphoreType.REGULAR,
             pltpu.SemaphoreType.DMA((ns,)),
-            pltpu.SemaphoreType.DMA((ns,)),
-            pltpu.SemaphoreType.DMA((fl_count * ns,)),
-            pltpu.SemaphoreType.DMA((nf * ch_out,)),
+            pltpu.SemaphoreType.DMA((1,)),
+            pltpu.SemaphoreType.DMA((1,)),
+            pltpu.SemaphoreType.DMA((1,)),
         ],
         compiler_params=pltpu.CompilerParams(
             collective_id=0, has_side_effects=True, vmem_limit_bytes=60 * 1024 * 1024

time: 23 us -> 21.7 us (0.943)
  the two profiles are of different devices: /device:TPU:7 before, /device:TPU:0 now
where the time goes in v2:
time: 21.7 us; the launch traced here: 21.5 us
  Pallas kernels  20.8 us (96%)
  local copies, waits for them, and re-layouts  0.71 us (3%)
    pallas_call x1, Pallas kernels, shards(): pl.pallas_call(functools.partial(kernel, nf, ns, rows, spec), out_shape=p...  20.8 us
    unnamed x1, local copies, waits for them, and re-layouts  0.71 us

profile of v2, /device:TPU:0, one launch (start us, length us, event | category | flops | bytes accessed | tf_op | source)
XLA Modules:
  0.0 21.5 jit_solution(7399500782228634637)
XLA Ops:
  0.0 20.8 %shard_map.55 = bf16[2,32,2,1024]{3,2,1,0:T(2,128)(2,1)S(1)} custom-call(bf16[32,48,128]{2,1,0:T(8,128)(2,1)} %bitcast.6, f32[1,128]{1,0:T(1,128)} %bitcast.7, f32[2,128,128]{2,1,0:T(8,128)} %constant.2.clone.trig_hbm, s32[8]{0:T(128)} %god_hbm.1, s32[8,8]{1,0:T(8,128)} %own_hbm.1), custom_call_target="tpu_custom_call" | custom-call | tf_op jit(solution)/shard_map/pallas_call | solution.py:311
  20.8 0.7 %copy.8 = bf16[2,32,1,2,1024]{4,3,2,1,0:T(2,128)(2,1)} copy(bf16[2,32,1,2,1024]{4,3,2,1,0:T(2,128)(2,1)S(1)} %bitcast.5) | data formatting | bytes 524288

commit v3 on v2

--- a/solution.py
+++ b/solution.py
@@ -11,20 +11,27 @@
 
 AVG = 16
 LANES = 128
-LEAD = 3
-HOLD = 1
-SLOW_EIGHTHS = (4, 3, 5, 2, 1, 6, 7)
-FAST_EIGHTHS = (4, 5, 3, 2, 6, 1, 7)
+PLANES = 4
+PLANS = (
+    (
+        ((1, 0), 'h2', (2, 0), 'h3', (3, 0), (3, 1), (1, 1), (2, 1), (0, 1), (0, 0), ('tell', 3)),
+        ((1, 0), 'h2', 'h3', 'wait', (1, 1), (2, 0), (3, 0), (3, 1), (2, 1), (0, 0), (0, 1)),
+    ),
+    (
+        ((2, 1), 'h2', (3, 0), (3, 1), (2, 0), (0, 0), (1, 1), (0, 1), (1, 0), ('tell', 3)),
+        ((2, 1), 'h2', 'wait', (3, 1), (3, 0), (2, 0), (0, 0), (0, 1), (1, 1), (1, 0)),
+    ),
+    (
+        ((2, 1), 'h2', (3, 1), (3, 0), (2, 0), (0, 0), (0, 1), (1, 1), (1, 0)),
+        ((2, 1), 'h2', (3, 1), (3, 0), (2, 0), (0, 0), (1, 1), (0, 1), (1, 0)),
+    ),
+    (
+        ((1, 0), 'h2', (2, 0), 'h3', (3, 0), (3, 1), (1, 1), (2, 1), (0, 1), (0, 0)),
+        ((1, 0), 'h2', (2, 0), 'h3', (3, 0), (3, 1), (1, 1), (2, 1), (0, 1), (0, 0)),
+    ),
+)
 MESH = pl.DeviceIdType.MESH
 OUT_SPACE = pltpu.VMEM
-
-
-def orders(ns):
-    plans = []
-    for eighths in (SLOW_EIGHTHS, FAST_EIGHTHS):
-        plan = [e * ns // 8 + k for e in eighths for k in range(ns // 8)]
-        plans.append(plan + [off for off in range(1, ns) if off not in plan])
-    return plans
 
 
 def deal_blocks(blocks, width):
@@ -46,7 +53,7 @@
     out_ref,
     x_ref, w_ref, trig_ref, god_ref, own_ref,
     xf, send1, held, left, vis, tiles, mixed, send2, dev_of, table,
-    lsem, row_sem, twin_sem, ssem1, rsem1, ssem2, rsem2,
+    lsem, row_sem, hop_sem, twin_sem, ssem1, rsem1, ssem2, rsem2,
 ):
     length = LANES
     ch_out = length // AVG
@@ -55,36 +62,49 @@
     fl_count = ch_out // rpf
     chunks = spec // ch_out
     step = 2 * ch_out
+    lanes = ns // PLANES
     b = lax.axis_index("freq")
     me = lax.axis_index("stn")
+    plane = me // lanes
+    lane = lax.rem(me, lanes)
 
     def load(n, src, dst):
         return pltpu.make_async_copy(src, dst, lsem.at[n])
 
     def load_x(th):
-        return load(4 + th, x_hbm.at[:, th * step : (th + 1) * step, :], x_ref.at[th])
+        return load(4, x_hbm.at[:, th * step : (th + 1) * step, :], x_ref.at[th])
 
     load_w = load(0, w_hbm, w_ref)
     load_trig = load(1, trig_hbm, trig_ref)
     load_god = load(2, god_hbm, god_ref)
     load_own = load(3, own_hbm, own_ref)
+
+    barrier = pltpu.get_barrier_semaphore()
+    def mate(delta, r):
+        return (plane + delta) * lanes + lax.rem(lane + r, lanes)
+
+    def greet(delta):
+        for r in range(lanes):
+            if delta or r:
+                pl.semaphore_signal(
+                    barrier, inc=1, device_id=(b, mate(delta, r)), device_id_type=MESH
+                )
+
+    for delta in (1, -1):
+        far = plane + delta
+        pl.when(jnp.logical_and(far >= 0, far < PLANES))(functools.partial(greet, delta))
+    greet(0)
+    for off in range(1, nf):
+        pl.semaphore_signal(
+            barrier, inc=1, device_id=(lax.rem(b + off, nf), me), device_id_type=MESH
+        )
+
     load_w.start()
     load_trig.start()
     for th in range(chunks):
         load_x(th).start()
     load_god.start()
     load_own.start()
-
-    barrier = pltpu.get_barrier_semaphore()
-    offsets = sorted(range(1, ns), key=lambda o: abs(o - ns / 2))
-    for off in offsets:
-        pl.semaphore_signal(
-            barrier, inc=1, device_id=(b, lax.rem(me + off, ns)), device_id_type=MESH
-        )
-    for off in range(1, nf):
-        pl.semaphore_signal(
-            barrier, inc=1, device_id=(lax.rem(b + off, nf), me), device_id_type=MESH
-        )
 
     load_w.wait()
     load_trig.wait()
@@ -97,8 +117,7 @@
     high = matrix.astype(jnp.bfloat16)
     low = (matrix - high.astype(jnp.float32)).astype(jnp.bfloat16)
 
-    for th in range(chunks):
-        load_x(th).wait()
+    load(4, x_ref, x_ref).wait()
     for th in range(chunks):
         xf[th] = x_ref[th].astype(jnp.float32).reshape(rows * step, length)
     for th in range(chunks):
@@ -133,29 +152,57 @@
             device_id_type=MESH,
         )
 
-    pl.semaphore_wait(barrier, ns - 1 + nf - 1)
-    def start_first(offs):
-        for off in offs:
-            first_copy(lax.rem(me + off, ns), me).start()
-
-    def end_first(offs):
-        for off in offs:
-            first_copy(lax.rem(me + off, ns), me).wait_send()
-
-    slow = lax.rem(b, 2) == 0
-    slow_order, fast_order = orders(ns)
-
-    @pl.when(slow)
-    def _():
-        start_first(slow_order)
-        end_first(slow_order[:LEAD])
-        pl.semaphore_signal(twin_sem, inc=1, device_id=(b + 1, me), device_id_type=MESH)
-
-    @pl.when(jnp.logical_not(slow))
-    def _():
-        start_first(fast_order[:HOLD])
-        pl.semaphore_wait(twin_sem, 1)
-        start_first(fast_order[HOLD:])
+    def tell(distance, delta):
+        pl.semaphore_signal(
+            hop_sem.at[2 * (distance - 2) + (delta < 0)], inc=1,
+            device_id=(b, mate(-delta, 0)), device_id_type=MESH,
+        )
+
+    def hear(distance, delta):
+        pl.semaphore_wait(hop_sem.at[2 * (distance - 2) + (delta < 0)], 1)
+
+    def targets(at, entry):
+        to = entry[0] if 2 * at < PLANES else PLANES - 1 - entry[0]
+        return [mate(to - at, r) for r in range(entry[1], lanes, 2) if to != at or r]
+
+    def is_send(entry):
+        return isinstance(entry, tuple) and entry[0] != "tell"
+
+    def each_role(run):
+        for at in range(PLANES):
+            inner = 0 < at < PLANES - 1
+            for half in range(2):
+                pl.when(jnp.logical_and(plane == at, lax.rem(b, 2) == half))(
+                    functools.partial(run, at, inner, PLANS[at][half])
+                )
+
+    def send_first(at, inner, plan):
+        up = 1 if 2 * at < PLANES else -1
+        pl.semaphore_wait(barrier, (3 if inner else 2) * lanes - 1 + nf - 1)
+        if inner:
+            tell(2, up)
+            tell(2, -up)
+        for entry in plan:
+            if entry == "h2":
+                hear(2, up)
+                if inner:
+                    tell(3, up)
+            elif entry == "h3":
+                hear(3, up)
+            elif entry == "wait":
+                pl.semaphore_wait(twin_sem, 1)
+            elif is_send(entry):
+                for d in targets(at, entry):
+                    first_copy(d, me).start()
+            else:
+                for sent in list(filter(is_send, plan))[: entry[1]]:
+                    for d in targets(at, sent):
+                        first_copy(d, me).wait_send()
+                pl.semaphore_signal(
+                    twin_sem, inc=1, device_id=(b + 1 - 2 * lax.rem(b, 2), me), device_id_type=MESH
+                )
+
+    each_role(send_first)
 
     for off in range(1, nf):
         pl.semaphore_signal(
@@ -284,8 +331,13 @@
         own.start()
         own.wait()
 
-    pl.when(slow)(lambda: end_first(slow_order[LEAD:]))
-    pl.when(jnp.logical_not(slow))(lambda: end_first(fast_order))
+    def end_first(at, inner, plan):
+        done = sum(entry[1] for entry in plan if not is_send(entry) and entry[0] == "tell")
+        for entry in list(filter(is_send, plan))[done:]:
+            for d in targets(at, entry):
+                first_copy(d, me).wait_send()
+
+    each_role(end_first)
 
     def end_second(count):
         whole(send2.at[:count], ssem2).wait()
@@ -329,8 +381,9 @@
             pltpu.VMEM((fl_count * ns, 2, rpf, sub * LANES), jnp.bfloat16),
             pltpu.SMEM((ns,), jnp.int32),
             pltpu.SMEM((ch_out * ns,), jnp.int32),
-            pltpu.SemaphoreType.DMA((4 + chunks,)),
+            pltpu.SemaphoreType.DMA((5,)),
             pltpu.SemaphoreType.REGULAR,
+            pltpu.SemaphoreType.REGULAR((2 * (PLANES - 2),)),
             pltpu.SemaphoreType.REGULAR,
             pltpu.SemaphoreType.DMA((ns,)),
             pltpu.SemaphoreType.DMA((1,)),

time: 21.7 us -> 21.6 us (level)
  no operation moved by 1% of the time
where the time goes in v3:
time: 21.6 us; the launch traced here: 21.4 us
  Pallas kernels  20.6 us (95%)
  local copies, waits for them, and re-layouts  0.71 us (3%)
    pallas_call x1, Pallas kernels, shards(): pl.pallas_call(functools.partial(kernel, nf, ns, rows, spec), out_shape=p...  20.6 us
    unnamed x1, local copies, waits for them, and re-layouts  0.71 us

profile of v3, /device:TPU:0, one launch (start us, length us, event | category | flops | bytes accessed | tf_op | source)
XLA Modules:
  0.0 21.4 jit_solution(8903297461350560383)
XLA Ops:
  0.0 20.6 %shard_map.55 = bf16[2,32,2,1024]{3,2,1,0:T(2,128)(2,1)S(1)} custom-call(bf16[32,48,128]{2,1,0:T(8,128)(2,1)} %bitcast.6, f32[1,128]{1,0:T(1,128)} %bitcast.7, f32[2,128,128]{2,1,0:T(8,128)} %constant.2.clone.trig_hbm, s32[8]{0:T(128)} %god_hbm.1, s32[8,8]{1,0:T(8,128)} %own_hbm.1), custom_call_target="tpu_custom_call" | custom-call | tf_op jit(solution)/shard_map/pallas_call | solution.py:363
  20.7 0.7 %copy.8 = bf16[2,32,1,2,1024]{4,3,2,1,0:T(2,128)(2,1)} copy(bf16[2,32,1,2,1024]{4,3,2,1,0:T(2,128)(2,1)S(1)} %bitcast.5) | data formatting | bytes 524288

commit v4 on v3

--- a/solution.py
+++ b/solution.py
@@ -109,8 +109,11 @@
     load_w.wait()
     load_trig.wait()
     weights = jnp.broadcast_to(w_ref[...], (length, length)).T * (1.0 / math.sqrt(length))
-    cosine = weights * trig_ref[0]
-    sine = weights * trig_ref[1]
+    odd = lax.rem(lax.broadcasted_iota(jnp.int32, (length // 2, length), 1), 2) == 1
+    cosine, sine = (
+        weights * jnp.concatenate([part, jnp.where(odd, -part, part)], axis=0)
+        for part in (trig_ref[0], trig_ref[1])
+    )
     matrix = jnp.concatenate(
         [jnp.concatenate([cosine, -sine], axis=1), jnp.concatenate([sine, cosine], axis=1)], axis=0
     )
@@ -356,7 +359,7 @@
     sub = rows // per_tile
     chunks = spec // ch_out
     index = np.arange(length)
-    theta = (index[:, None] * index[None, :] % length) * (2.0 * math.pi / length)
+    theta = (index[: length // 2, None] * index[None, :] % length) * (2.0 * math.pi / length)
     trig = jnp.asarray(np.stack([np.cos(theta), np.sin(theta)]), jnp.float32)
     x = samples.reshape(rows, spec * 2, length)
     hbm = pl.BlockSpec(memory_space=pltpu.HBM)
@@ -368,7 +371,7 @@
         scratch_shapes=[
             pltpu.VMEM((chunks, rows, 2 * ch_out, length), jnp.bfloat16),
             pltpu.VMEM((1, length), jnp.float32),
-            pltpu.VMEM((2, length, length), jnp.float32),
+            pltpu.VMEM((2, length // 2, length), jnp.float32),
             pltpu.SMEM((ns,), jnp.int32),
             pltpu.SMEM((ns, ns), jnp.int32),
             pltpu.VMEM((chunks, rows * 2 * ch_out, length), jnp.float32),

time: 21.6 us -> 21.6 us (level)
  no operation moved by 1% of the time
where the time goes in v4:
time: 21.6 us; the launch traced here: 21.3 us
  Pallas kernels  20.6 us (95%)
  local copies, waits for them, and re-layouts  0.71 us (3%)
    pallas_call x1, Pallas kernels, shards(): pl.pallas_call(functools.partial(kernel, nf, ns, rows, spec), out_shape=p...  20.6 us
    unnamed x1, local copies, waits for them, and re-layouts  0.71 us

profile of v4, /device:TPU:0, one launch (start us, length us, event | category | flops | bytes accessed | tf_op | source)
XLA Modules:
  0.0 21.3 jit_solution(451274697318452533)
XLA Ops:
  0.0 20.6 %shard_map.55 = bf16[2,32,2,1024]{3,2,1,0:T(2,128)(2,1)S(1)} custom-call(bf16[32,48,128]{2,1,0:T(8,128)(2,1)} %bitcast.6, f32[1,128]{1,0:T(1,128)} %bitcast.7, f32[2,64,128]{2,1,0:T(8,128)} %constant.2.clone.trig_hbm, s32[8]{0:T(128)} %god_hbm.1, s32[8,8]{1,0:T(8,128)} %own_hbm.1), custom_call_target="tpu_custom_call" | custom-call | tf_op jit(solution)/shard_map/pallas_call | solution.py:366
  20.6 0.7 %copy.8 = bf16[2,32,1,2,1024]{4,3,2,1,0:T(2,128)(2,1)} copy(bf16[2,32,1,2,1024]{4,3,2,1,0:T(2,128)(2,1)S(1)} %bitcast.5) | data formatting | bytes 524288

commit v5 on v4

--- a/solution.py
+++ b/solution.py
@@ -103,8 +103,6 @@
     load_trig.start()
     for th in range(chunks):
         load_x(th).start()
-    load_god.start()
-    load_own.start()
 
     load_w.wait()
     load_trig.wait()
@@ -206,6 +204,8 @@
                 )
 
     each_role(send_first)
+    load_god.start()
+    load_own.start()
 
     for off in range(1, nf):
         pl.semaphore_signal(

time: 21.6 us -> 21.6 us (level)
  no operation moved by 1% of the time
where the time goes in v5:
time: 21.6 us; the launch traced here: 21.3 us
  Pallas kernels  20.6 us (95%)
  local copies, waits for them, and re-layouts  0.71 us (3%)
    pallas_call x1, Pallas kernels, shards(): pl.pallas_call(functools.partial(kernel, nf, ns, rows, spec), out_shape=p...  20.6 us
    unnamed x1, local copies, waits for them, and re-layouts  0.71 us

profile of v5, /device:TPU:0, one launch (start us, length us, event | category | flops | bytes accessed | tf_op | source)
XLA Modules:
  0.0 21.3 jit_solution(6477422211401633094)
XLA Ops:
  0.0 20.6 %shard_map.55 = bf16[2,32,2,1024]{3,2,1,0:T(2,128)(2,1)S(1)} custom-call(bf16[32,48,128]{2,1,0:T(8,128)(2,1)} %bitcast.6, f32[1,128]{1,0:T(1,128)} %bitcast.7, f32[2,64,128]{2,1,0:T(8,128)} %constant.2.clone.trig_hbm, s32[8]{0:T(128)} %god_hbm.1, s32[8,8]{1,0:T(8,128)} %own_hbm.1), custom_call_target="tpu_custom_call" | custom-call | tf_op jit(solution)/shard_map/pallas_call | solution.py:366
  20.6 0.7 %copy.8 = bf16[2,32,1,2,1024]{4,3,2,1,0:T(2,128)(2,1)} copy(bf16[2,32,1,2,1024]{4,3,2,1,0:T(2,128)(2,1)S(1)} %bitcast.5) | data formatting | bytes 524288
